TPU v7x, 512 devices: a whole 4x8x8 slice. The times are simulated.
512 devices in a mesh: gx: 4 (over y_lo), gy: 16 (over y_hi, z), gz: 8 (over x, core).
Axes of the slice: x: 4, y: 8 (y_hi: 2, y_lo: 4; y = y_hi * 4 + y_lo), z: 8, core: 2. Of those that a mesh axis runs over, the one named last changes fastest.
Arguments:
- grads: float32 [4, 16, 8, 160, 4096], P('gx', 'gy', 'gz'), may hold values from -6 to 6
- peer_table: int32 [16], replicated, may hold values from 0 to 15, each once
- layer_offsets: int32 [2], replicated, may hold values from 0 to 96, as said below
Outputs:
- averaged: float32 [4, 16, 8, 128, 4096], P('gx', 'gy', 'gz')
Inputs may be any that keep to these rules, and one draw needn't show every extreme that they name: layer_offsets[l] is a multiple of 8 between l * (80) and l * 80 + 16; the last layer's offset is the largest of these.
All inputs are finite; a program needn't handle non-finite values.
Results may differ from a plain program's by a relative error of at most 0.00002.
Values sent between devices are 32-bit elements; how exact they have to be, the bound alone decides.
No kernel may reach another device: no remote copies, remote signals or barrier semaphores. Data moves between devices by JAX's collectives and lax.ppermute only.
A program may use at most 64 MiB of HBM per device.

v0:
```python
import jax
import jax.numpy as jnp
from jax import lax
from jax.sharding import PartitionSpec as P

ROWS = 64
LAYERS = 2


def filled_up(lines, peers):
    spare = -lines.shape[0] % peers
    if not spare:
        return lines
    return jnp.concatenate([lines, jnp.zeros((spare, *lines.shape[1:]), lines.dtype)])


def sum_by_parts(shard, axis):
    lines = shard.reshape(-1, *shard.shape[1:][-1:])
    own = lax.psum_scatter(
        filled_up(lines, lax.axis_size(axis)), axis, scatter_dimension=0, tiled=True
    )
    whole = lax.all_gather(own, axis).reshape(-1, *lines.shape[1:])
    return lax.slice_in_dim(whole, 0, len(lines)).reshape(shard.shape)


def on_device(grads, peer_table, layer_offsets):
    buffer = grads[0, 0, 0]
    pieces = [lax.dynamic_slice_in_dim(buffer, layer_offsets[i], ROWS, 0) for i in range(LAYERS)]
    packed = jnp.concatenate(pieces, axis=0)
    count_y = lax.axis_size("gy")
    group_b = min(8, count_y)
    group_a = lax.axis_size("gx") * (count_y // group_b)
    places = jnp.arange(count_y, dtype=jnp.int32)
    onehot = (peer_table[:, None] == places[None, :]).astype(jnp.int32)
    inverse = jnp.sum(onehot * places[:, None], axis=0)
    spread = lax.all_to_all(packed[None], "gy", split_axis=1, concat_axis=0, tiled=True)
    current = jnp.take(spread, peer_table, axis=0)
    total_c = sum_by_parts(current, "gz")
    current = 0.5 * current + 0.5 / lax.axis_size("gz") * total_c
    block_rows = current.shape[1]
    width = current.shape[2]
    split = current.reshape(count_y // group_b, group_b, block_rows, width)
    total_b = jnp.sum(split, axis=1, keepdims=True)
    split = 0.5 * split + 0.5 / group_b * total_b
    local_a = jnp.sum(split, axis=0, keepdims=True)
    total_a = lax.psum(local_a, "gx")
    split = 0.5 * split + 0.5 / group_a * total_a
    current = jnp.take(split.reshape(count_y, block_rows, width), inverse, axis=0)
    result = lax.all_to_all(current, "gy", split_axis=0, concat_axis=1, tiled=True)[0]
    return result[None, None, None]


def solution(mesh):
    placed = (P("gx", "gy", "gz", None, None), P(), P())
    return jax.shard_map(
        on_device,
        mesh=mesh,
        in_specs=placed,
        out_specs=P("gx", "gy", "gz", None, None),
        check_vma=False,
    )
```

profile of v0, /device:TPU:1, one launch (start us, length us, event | category | flops | bytes accessed | tf_op | source)
XLA Modules:
  0.0 327.0 jit_solution(8673940467536958085)
XLA Ops:
  6.5 1.4 fusion.2
  11.8 1.8 dynamic-slice_bitcast_fusion.1
  13.6 0.1 pad_maximum_fusion
  13.7 3.7 %broadcast_in_dim.19 = f32[1,128,4096]{2,0,1:T(1,128)} reshape(f32[128,4096]{1,0:T(8,128)S(1)} %pad_maximum_fusion) | data formatting | bytes 4194304 | tf_op jit(solution)/shard_map/broadcast_in_dim | solution.py:36
  17.4 16.4 %all-to-all-start = ((f32[1,128,4096]{2,0,1:T(1,128)}), f32[1,128,4096]{2,0,1:T(1,128)S(1)}, u32[]{:S(2)}, u32[]{:S(2)}) async-start(f32[1,128,4096]{2,0,1:T(1,128)} %broadcast_in_dim.19), calls=%async_computation | async-start | bytes 4194304 | tf_op jit(solution)/shard_map/all_to_all | solution.py:36
  33.8 0.0 reduce-scatter.2.cloned.1.call-start
  33.9 0.0 copy-done.2
  33.9 53.5 %all-to-all-done = f32[1,128,4096]{2,0,1:T(1,128)S(1)} async-done(((f32[1,128,4096]{2,0,1:T(1,128)}), f32[1,128,4096]{2,0,1:T(1,128)S(1)}, u32[]{:S(2)}, u32[]{:S(2)}) %all-to-all-start) | async-done | bytes 2097184 | tf_op jit(solution)/shard_map/all_to_all | solution.py:36
  87.4 3.0 copy.6
  90.4 2.3 gather_fusion
  92.6 1.6 select_bitcast_fusion
  94.2 0.0 reduce-scatter.2.cloned.1.call-update
  94.2 0.0 all-gather.3.cloned.1.call-start
  94.3 49.6 %reduce-scatter.2.cloned.1.call-done = f32[16,4096]{1,0:T(8,128)} async-done(((f32[128,4096]{1,0:T(8,128)}), f32[16,4096]{1,0:T(8,128)}) %reduce-scatter.2.cloned.1.call-update) | async-done | bytes 262160 | tf_op jit(solution)/shard_map/reduce_scatter | solution.py:19
  143.9 0.0 all-gather.3.cloned.1.call-update
  143.9 0.0 all-reduce.2.cloned.1.call-start
  144.0 33.7 %all-gather.3.cloned.1.call-done = f32[128,4096]{1,0:T(8,128)} async-done(((f32[16,4096]{1,0:T(8,128)}), f32[128,4096]{1,0:T(8,128)}) %all-gather.3.cloned.1.call-update) | async-done | bytes 2097168 | tf_op jit(solution)/shard_map/all_gather | solution.py:22
  177.7 2.1 bitcast_reduce_fusion
  179.8 0.0 copy-start
  179.8 1.3 copy-done
  181.1 0.2 fusion.1
  181.3 1.2 reduce_sum.28
  182.6 0.0 all-reduce.2.cloned.1.call-update
  182.6 0.1 select_reduce_fusion
  182.7 68.9 %all-reduce.2.cloned.1.call-done = f32[1,8,8,4096]{3,2,1,0:T(8,128)} async-done(((f32[1,8,8,4096]{3,2,1,0:T(8,128)}), f32[1,8,8,4096]{3,2,1,0:T(8,128)}) %all-reduce.2.cloned.1.call-update) | async-done | bytes 1048592 | tf_op jit(solution)/shard_map/psum | solution.py:46
  251.6 1.3 multiply_bitcast_fusion
  252.9 0.0 copy-done.1
  252.9 1.6 bitcast_add_fusion
  254.5 2.3 gather_fusion.1
  256.8 0.3 broadcast_select_fusion
  257.0 62.1 %all_to_all.21 = f32[16,8,4096]{2,1,0:T(8,128)S(1)} all-to-all(f32[16,8,4096]{2,1,0:T(8,128)S(1)} %broadcast_select_fusion), channel_id=1, replica_groups=mesh['gx'=4,'gy'=16,'gz'=8] {'gy'}, dimensions={0} | all-to-all | bytes 4194304 | tf_op jit(solution)/shard_map/all_to_all | solution.py:49
  319.2 1.3 copy.9
  (9 shorter events, 0.1 us)
Async XLA Ops:
  17.4 16.4 %copy-start.2 = (s32[16]{0:T(128)S(1)}, s32[16]{0:T(128)}, u32[]{:S(2)}) copy-start(s32[16]{0:T(128)} %param.6) | copy-start | bytes 196
  17.4 70.0 %all-to-all-start = ((f32[1,128,4096]{2,0,1:T(1,128)}), f32[1,128,4096]{2,0,1:T(1,128)S(1)}, u32[]{:S(2)}, u32[]{:S(2)}) async-start(f32[1,128,4096]{2,0,1:T(1,128)} %broadcast_in_dim.19), calls=%async_computation | async-start | bytes 4194304 | tf_op jit(solution)/shard_map/all_to_all | solution.py:36
  33.8 110.1 %reduce-scatter.2.cloned.1.call-start = ((), (), s32[]{:S(2)}) async-start(), calls=%async_computation.3 | async-start | bytes 2359296 | tf_op jit(solution)/shard_map/reduce_scatter | solution.py:19
  94.2 83.4 %all-gather.3.cloned.1.call-start = ((), (), s32[]{:S(2)}) async-start(), calls=%async_computation.5 | async-start | bytes 2359296 | tf_op jit(solution)/shard_map/all_gather | solution.py:22
  143.9 107.6 %all-reduce.2.cloned.1.call-start = ((), (), s32[]{:S(2)}) async-start(), calls=%async_computation.4 | async-start | bytes 2097152 | tf_op jit(solution)/shard_map/psum | solution.py:46
  179.8 1.3 copy-start
  182.6 70.3 %copy-start.1 = (f32[16,8,4096]{2,1,0:T(8,128)S(1)}, f32[16,8,4096]{2,1,0:T(8,128)}, u32[]{:S(2)}) copy-start(f32[16,8,4096]{2,1,0:T(8,128)} %copy-done) | copy-start | bytes 6291460
Sparse Core Ops, SparseCore 0:
  94.4 49.4 reduce-scatter.1
  146.1 31.5 all-gather.2
  182.7 68.8 all-reduce.1
where the time goes:
time: 329 us; the launch traced here: 327 us
  waiting for transfers between devices  206 us (63%)
  blocking collectives  62.1 us (19%)
  between operations  17.1 us (5%)
  local copies, waits for them, and re-layouts  17 us (5%)
  starting transfers between devices  16.5 us (5%)
  other arithmetic  8.57 us (3%)
    psum x1, waiting for transfers between devices, on_device(): total_a = lax.psum(local_a, 'gx')  68.9 us
    all_to_all x1, blocking collectives, on_device(): lax.all_to_all(current, 'gy', split_axis=0, concat_axis=1, tiled=True)[0]  62.1 us
    all_to_all x1, waiting for transfers between devices, on_device(): lax.all_to_all(packed[None], 'gy', split_axis=1, concat_axis=0, tiled=True)  53.5 us
    reduce_scatter x1, waiting for transfers between devices, sum_by_parts(): lax.psum_scatter(filled_up(lines, lax.axis_size(axis)), axis, scatter_dim...  49.6 us
    all_gather x1, waiting for transfers between devices, sum_by_parts(): whole = lax.all_gather(own, axis).reshape(-1, *lines.shape[1:])  33.7 us
    all_to_all x1, starting transfers between devices, on_device(): lax.all_to_all(packed[None], 'gy', split_axis=1, concat_axis=0, tiled=True)  16.4 us
  transfers between devices with their start and end apart: 4, of which 4 were waited for; matrix products, arithmetic and copies ran while one was open for 0% of the time, Pallas kernels for 0%

commit v1 on v0

v1 whole, which is shorter than its diff:
```python
import jax
import jax.numpy as jnp
from jax import lax
from jax.experimental import pallas as pl
from jax.experimental.pallas import tpu as pltpu
from jax.sharding import PartitionSpec as P

ROWS = 64
LAYERS = 2
GB = 8
SUB = 8
LANE = 128
AXES = ("gx", "gy", "gz")
VMEM = pl.BlockSpec(memory_space=pltpu.VMEM)
SMEM = pl.BlockSpec(memory_space=pltpu.SMEM)
ANY = pl.BlockSpec(memory_space=pl.ANY)
HBM = pl.BlockSpec(memory_space=pltpu.HBM)
SMALL = pltpu.CompilerParams(vmem_limit_bytes=8 * 1024 * 1024)


def pack_kernel(offsets, grads, out, sem):
    columns, lines, lane = out.shape
    copies = []
    for layer in range(LAYERS):
        start = pl.multiple_of(offsets[layer], SUB)
        for c in range(columns):
            copies.append(
                pltpu.make_async_copy(
                    grads.at[0, 0, 0, pl.ds(start, ROWS), pl.ds(c * lane, lane)],
                    out.at[c, pl.ds(layer * ROWS, ROWS), :],
                    sem,
                )
            )
    for copy in copies:
        copy.start()
    pltpu.make_async_copy(out, out, sem).wait()


def mix_kernel(table, spread, out, mixed_c, sum_b):
    n_i, n_p, n_k = spread.shape[:3]
    upper = n_p // GB
    group_a = n_i * upper

    def round_c(n, _):
        i, p = n // n_p, n % n_p
        block = spread[i, p]
        mixed_c[i, p] = 0.5 * block + (0.5 / n_k) * jnp.sum(block, axis=0, keepdims=True)
        return _

    lax.fori_loop(0, n_i * n_p, round_c, 0, unroll=4)

    def round_b(n, _):
        i, h = n // upper, n % upper
        total = mixed_c[i, table[h * GB]]
        for g in range(1, GB):
            total = total + mixed_c[i, table[h * GB + g]]
        sum_b[i, h] = total * (0.5 / GB)
        return _

    lax.fori_loop(0, n_i * upper, round_b, 0)

    def round_a(g, _):
        total = None
        for i in range(n_i):
            for h in range(upper):
                mixed_b = 0.5 * mixed_c[i, table[h * GB + g]] + sum_b[i, h]
                total = mixed_b if total is None else total + mixed_b
        total = total * (0.5 / group_a)
        for i in range(n_i):
            for h in range(upper):
                p = table[h * GB + g]
                mixed_b = 0.5 * mixed_c[i, p] + sum_b[i, h]
                out[i, p] = 0.5 * mixed_b + total
        return _

    lax.fori_loop(0, GB, round_a, 0)


def unpack_kernel(tiles, out, sem):
    columns, lines, lane = tiles.shape
    copies = [
        pltpu.make_async_copy(tiles.at[c], out.at[0, 0, 0, :, pl.ds(c * lane, lane)], sem)
        for c in range(columns)
    ]
    for copy in copies:
        copy.start()
    pltpu.make_async_copy(tiles, tiles, sem).wait()


def on_device(grads, peer_table, layer_offsets):
    n_i, n_p, n_k = (lax.axis_size(a) for a in AXES)
    peers = n_i * n_p * n_k
    width = grads.shape[-1]
    columns = width // LANE
    lines = ROWS * LAYERS
    tiles = pl.pallas_call(
        pack_kernel,
        out_shape=jax.ShapeDtypeStruct((columns, lines, LANE), jnp.float32),
        in_specs=[SMEM, HBM],
        out_specs=ANY,
        scratch_shapes=[pltpu.SemaphoreType.DMA],
        compiler_params=SMALL,
        name="pack",
    )(layer_offsets, grads)
    spread = lax.all_to_all(
        tiles.reshape(peers, -1, LANE), AXES, split_axis=0, concat_axis=0, tiled=True
    )
    per = spread.shape[1]
    block = (n_i, n_p, n_k, per, LANE)
    mixed = pl.pallas_call(
        mix_kernel,
        out_shape=jax.ShapeDtypeStruct(block, jnp.float32),
        in_specs=[SMEM, VMEM],
        out_specs=VMEM,
        scratch_shapes=[
            pltpu.VMEM(block, jnp.float32),
            pltpu.VMEM((n_i, n_p // GB, n_k, per, LANE), jnp.float32),
        ],
        compiler_params=SMALL,
        name="mix",
    )(peer_table, spread.reshape(block))
    back = lax.all_to_all(
        mixed.reshape(peers, per, LANE), AXES, split_axis=0, concat_axis=0, tiled=True
    )
    return pl.pallas_call(
        unpack_kernel,
        out_shape=jax.ShapeDtypeStruct((1, 1, 1, lines, width), jnp.float32),
        in_specs=[ANY],
        out_specs=ANY,
        scratch_shapes=[pltpu.SemaphoreType.DMA],
        compiler_params=SMALL,
        name="unpack",
    )(back.reshape(columns, lines, LANE))


def solution(mesh):
    placed = (P("gx", "gy", "gz", None, None), P(), P())
    return jax.shard_map(
        on_device,
        mesh=mesh,
        in_specs=placed,
        out_specs=P("gx", "gy", "gz", None, None),
        check_vma=False,
    )
```

time: 329 us -> 148 us (0.45)
  waiting for transfers between devices: 206 us -> 0 us
  blocking collectives: 62.1 us -> 141 us
  between operations: 17.1 us -> 0.03 us
  starting transfers between devices: 16.5 us -> 0 us
  local copies, waits for them, and re-layouts: 17 us -> 2.4 us
  other arithmetic: 8.57 us -> 0 us
  Pallas kernels: 0 us -> 4.29 us
    all_to_all x1 -> x2, blocking collectives: 62.1 us -> 141 us  [the longest x1 76.6 us: on_device(): lax.all_to_all(tiles.reshape(peers, -1, LANE), AXES, split_axis=0, concat...]
    psum x1 -> x0, waiting for transfers between devices: 68.9 us -> none  [on_device(): total_a = lax.psum(local_a, 'gx')]
    all_to_all x1 -> x0, waiting for transfers between devices: 53.5 us -> none  [on_device(): lax.all_to_all(packed[None], 'gy', split_axis=1, concat_axis=0, tiled=True)]
    reduce_scatter x1 -> x0, waiting for transfers between devices: 49.6 us -> none  [sum_by_parts(): lax.psum_scatter(filled_up(lines, lax.axis_size(axis)), axis, scatter_dim...]
    all_gather x1 -> x0, waiting for transfers between devices: 33.7 us -> none  [sum_by_parts(): whole = lax.all_gather(own, axis).reshape(-1, *lines.shape[1:])]
    all_to_all x1 -> x0, starting transfers between devices: 16.4 us -> none  [on_device(): lax.all_to_all(packed[None], 'gy', split_axis=1, concat_axis=0, tiled=True)]
    gather x2 -> x0, local copies, waits for them, and re-layouts: 4.54 us -> none  [the longest x1 2.27 us: on_device(): current = jnp.take(spread, peer_table, axis=0)]
    pallas_call x0 -> x3, Pallas kernels: none -> 4.29 us  [the longest x1 2.04 us: on_device(): pl.pallas_call(mix_kernel, out_shape=jax.ShapeDtypeStruct(block, jnp.floa...]
  transfers between devices with their start and end apart: 4 -> 0, of which waited for: 4 -> 0; matrix products, arithmetic and copies ran while one was open for 0% -> 0% of each run, Pallas kernels for 0% -> 0%
where the time goes in v1:
time: 148 us
  blocking collectives  141 us (95%)
  Pallas kernels  4.29 us (3%)
  local copies, waits for them, and re-layouts  2.4 us (2%)
    all_to_all x1, blocking collectives, on_device(): lax.all_to_all(tiles.reshape(peers, -1, LANE), AXES, split_axis=0, concat...  76.6 us
    all_to_all x1, blocking collectives, on_device(): lax.all_to_all(mixed.reshape(peers, per, LANE), AXES, split_axis=0, conca...  64.2 us

profile of v1, /device:TPU:1, one launch (start us, length us, event | category | flops | bytes accessed | tf_op | source)
XLA Modules:
  0.0 147.6 jit_solution(15688501784373284277)
XLA Ops:
  0.0 0.0 copy-start
  0.0 1.7 %copy-done = f32[1,1,1,160,4096]{4,3,2,1,0:T(8,128)S(1)} copy-done((f32[1,1,1,160,4096]{4,3,2,1,0:T(8,128)S(1)}, f32[1,1,1,160,4096]{4,3,2,1,0:T(8,128)}, u32[]{:S(2)}) %copy-start) | copy-done | bytes 2621464
  1.7 0.0 copy-start.1
  1.7 0.7 copy-done.1
  2.4 1.0 pack.1
  3.4 0.0 copy-start.2
  3.4 76.6 %all_to_all.10 = f32[512,8,128]{2,1,0:T(8,128)S(1)} all-to-all(f32[512,8,128]{2,1,0:T(8,128)S(1)} %bitcast.4), channel_id=1, replica_groups=mesh['gx'=4,'gy'=16,'gz'=8] {'gx','gy','gz'}, dimensions={0} | all-to-all | bytes 4194304 | tf_op jit(solution)/shard_map/all_to_all | solution.py:105
  80.0 0.0 copy-done.2
  80.0 2.0 %mix.1 = f32[4,16,8,8,128]{4,3,2,1,0:T(8,128)S(1)} custom-call(s32[16]{0:T(128)S(1)} %copy-done.2, f32[4,16,8,8,128]{4,3,2,1,0:T(8,128)S(1)} %bitcast.5), custom_call_target="tpu_custom_call" | custom-call | tf_op jit(solution)/shard_map/mix/pallas_call | solution.py:110
  82.1 64.2 %all_to_all.11 = f32[512,8,128]{2,1,0:T(8,128)S(1)} all-to-all(f32[512,8,128]{2,1,0:T(8,128)S(1)} %bitcast.6), channel_id=1, replica_groups=mesh['gx'=4,'gy'=16,'gz'=8] {'gx','gy','gz'}, dimensions={0} | all-to-all | bytes 4194304 | tf_op jit(solution)/shard_map/all_to_all | solution.py:122
  146.3 1.3 unpack.1
Async XLA Ops:
  0.0 1.7 %copy-start = (f32[1,1,1,160,4096]{4,3,2,1,0:T(8,128)S(1)}, f32[1,1,1,160,4096]{4,3,2,1,0:T(8,128)}, u32[]{:S(2)}) copy-start(f32[1,1,1,160,4096]{4,3,2,1,0:T(8,128)} %grads.1) | copy-start | bytes 7864324
  1.7 0.7 copy-start.1
  3.4 76.7 %copy-start.2 = (s32[16]{0:T(128)S(1)}, s32[16]{0:T(128)}, u32[]{:S(2)}) copy-start(s32[16]{0:T(128)} %table.1) | copy-start | bytes 196

commit v2 on v1

v2 whole, which is shorter than its diff:
```python
import jax
import jax.numpy as jnp
from jax import lax
from jax.experimental import pallas as pl
from jax.experimental.pallas import tpu as pltpu
from jax.sharding import PartitionSpec as P

ROWS = 64
LAYERS = 2
GB = 8
SUB = 8
LANE = 128
AXES = ("gx", "gy", "gz")
VMEM = pl.BlockSpec(memory_space=pltpu.VMEM)
SMEM = pl.BlockSpec(memory_space=pltpu.SMEM)
ANY = pl.BlockSpec(memory_space=pl.ANY)
SMALL = pltpu.CompilerParams(vmem_limit_bytes=8 * 1024 * 1024)


def pack_kernel(offsets, grads, out, sem):
    for layer in range(LAYERS):
        start = pl.multiple_of(offsets[layer], SUB)
        pltpu.make_async_copy(
            grads.at[0, 0, 0, pl.ds(start, ROWS), :],
            out.at[pl.ds(layer * ROWS, ROWS), :],
            sem,
        ).start()
    pltpu.make_async_copy(out, out, sem).wait()


def mix_kernel(table, spread, out, quarter, sum_b):
    n_i, n_p, n_k = spread.shape[:3]
    upper = n_p // GB
    group_a = n_i * upper

    def rounds_c_b(n, _):
        i, h = n // upper, n % upper
        total = None
        for g in range(GB):
            block = spread[i, table[h * GB + g]]
            mixed = 0.125 * block + (0.125 / n_k) * jnp.sum(block, axis=0, keepdims=True)
            quarter[i, h * GB + g] = mixed
            total = mixed if total is None else total + mixed
        sum_b[i, h] = total * (1.0 / GB)
        return _

    lax.fori_loop(0, n_i * upper, rounds_c_b, 0)

    def round_a(g, _):
        for k in range(n_k):
            mixed = [
                quarter[i, h * GB + g, k] + sum_b[i, h, k] for i in range(n_i) for h in range(upper)
            ]
            total = mixed[0]
            for value in mixed[1:]:
                total = total + value
            total = total * (1.0 / group_a)
            for i in range(n_i):
                for h in range(upper):
                    out[i, table[h * GB + g], k] = mixed[i * upper + h] + total
        return _

    lax.fori_loop(0, GB, round_a, 0)


def on_device(grads, peer_table, layer_offsets):
    n_i, n_p, n_k = (lax.axis_size(a) for a in AXES)
    peers = n_i * n_p * n_k
    width = grads.shape[-1]
    columns = width // LANE
    lines = ROWS * LAYERS
    packed = pl.pallas_call(
        pack_kernel,
        out_shape=pltpu.VMEM((lines, width), jnp.float32),
        in_specs=[SMEM, ANY],
        out_specs=ANY,
        scratch_shapes=[pltpu.SemaphoreType.DMA],
        name="pack",
    )(layer_offsets, grads)
    tiles = packed.reshape(-1, SUB, columns, LANE).transpose(0, 2, 1, 3)
    spread = lax.all_to_all(
        tiles.reshape(peers, -1, LANE), AXES, split_axis=0, concat_axis=0, tiled=True
    )
    per = spread.shape[1]
    block = (n_i, n_p, n_k, per, LANE)
    mixed = pl.pallas_call(
        mix_kernel,
        out_shape=jax.ShapeDtypeStruct(block, jnp.float32),
        in_specs=[SMEM, VMEM],
        out_specs=VMEM,
        scratch_shapes=[
            pltpu.VMEM(block, jnp.float32),
            pltpu.VMEM((n_i, n_p // GB, n_k, per, LANE), jnp.float32),
        ],
        compiler_params=SMALL,
        name="mix",
    )(peer_table, spread.reshape(block))
    back = lax.all_to_all(
        mixed.reshape(peers, per, LANE), AXES, split_axis=0, concat_axis=0, tiled=True
    )
    tiles = back.reshape(-1, columns, SUB, LANE).transpose(0, 2, 1, 3)
    return tiles.reshape(1, 1, 1, lines, width)


def solution(mesh):
    placed = (P("gx", "gy", "gz", None, None), P(), P())
    return jax.shard_map(
        on_device,
        mesh=mesh,
        in_specs=placed,
        out_specs=P("gx", "gy", "gz", None, None),
        check_vma=False,
    )
```

time: 148 us -> 146 us (0.986)
  no operation moved by 1% of the time
where the time goes in v2:
time: 146 us
  blocking collectives  141 us (97%)
  Pallas kernels  3.65 us (2%)
    all_to_all x1, blocking collectives, on_device(): lax.all_to_all(tiles.reshape(peers, -1, LANE), AXES, split_axis=0, concat...  76.6 us
    all_to_all x1, blocking collectives, on_device(): lax.all_to_all(mixed.reshape(peers, per, LANE), AXES, split_axis=0, conca...  64.2 us

profile of v2, /device:TPU:1, one launch (start us, length us, event | category | flops | bytes accessed | tf_op | source)
XLA Modules:
  0.0 145.9 jit_solution(4249321896892711049)
XLA Ops:
  0.0 2.2 %pack.1 = f32[128,4096]{1,0:T(8,128)S(1)} custom-call(s32[2]{0:T(128)} %offsets.1, f32[1,1,1,160,4096]{4,3,2,1,0:T(8,128)} %grads.1), custom_call_target="tpu_custom_call" | custom-call | tf_op jit(solution)/shard_map/pack/pallas_call | solution.py:72
  2.2 0.0 copy-start
  2.2 76.6 %all_to_all.10 = f32[512,8,128]{2,1,0:T(8,128)S(1)} all-to-all(f32[512,8,128]{2,1,0:T(8,128)S(1)} %bitcast.12), channel_id=1, replica_groups=mesh['gx'=4,'gy'=16,'gz'=8] {'gx','gy','gz'}, dimensions={0} | all-to-all | bytes 4194304 | tf_op jit(solution)/shard_map/all_to_all | solution.py:81
  78.9 0.0 copy-done
  78.9 1.4 mix.1
  80.3 64.2 %all_to_all.11 = f32[512,8,128]{2,1,0:T(8,128)S(1)} all-to-all(f32[512,8,128]{2,1,0:T(8,128)S(1)} %bitcast.14), channel_id=1, replica_groups=mesh['gx'=4,'gy'=16,'gz'=8] {'gx','gy','gz'}, dimensions={0} | all-to-all | bytes 4194304 | tf_op jit(solution)/shard_map/all_to_all | solution.py:98
  144.6 1.3 copy.5
Async XLA Ops:
  2.2 76.7 %copy-start = (s32[16]{0:T(128)S(1)}, s32[16]{0:T(128)}, u32[]{:S(2)}) copy-start(s32[16]{0:T(128)} %table.1) | copy-start | bytes 196

commit v3 on v2

--- a/solution.py
+++ b/solution.py
@@ -3,6 +3,7 @@
 from jax import lax
 from jax.experimental import pallas as pl
 from jax.experimental.pallas import tpu as pltpu
+from jax.sharding import Mesh
 from jax.sharding import PartitionSpec as P
 
 ROWS = 64
@@ -10,7 +11,8 @@
 GB = 8
 SUB = 8
 LANE = 128
-AXES = ("gx", "gy", "gz")
+NEAR = 8
+AXES = ("gx", "gy_near", "gy_far", "gz")
 VMEM = pl.BlockSpec(memory_space=pltpu.VMEM)
 SMEM = pl.BlockSpec(memory_space=pltpu.SMEM)
 ANY = pl.BlockSpec(memory_space=pl.ANY)
@@ -28,43 +30,52 @@
     pltpu.make_async_copy(out, out, sem).wait()
 
 
-def mix_kernel(table, spread, out, quarter, sum_b):
+def mix_kernel(table, spread, out, part_c, part_b):
     n_i, n_p, n_k = spread.shape[:3]
     upper = n_p // GB
-    group_a = n_i * upper
+    far = n_p // NEAR
+
+    def slot(j):
+        p = table[j]
+        return lax.rem(p, NEAR) * far + lax.div(p, NEAR)
 
     def rounds_c_b(n, _):
         i, h = n // upper, n % upper
-        total = None
+        blocks, means = None, None
         for g in range(GB):
-            block = spread[i, table[h * GB + g]]
-            mixed = 0.125 * block + (0.125 / n_k) * jnp.sum(block, axis=0, keepdims=True)
-            quarter[i, h * GB + g] = mixed
-            total = mixed if total is None else total + mixed
-        sum_b[i, h] = total * (1.0 / GB)
+            block = spread[i, slot(h * GB + g)]
+            mean = (0.125 / n_k) * jnp.sum(block, axis=0)
+            part_c[i, h * GB + g] = mean
+            blocks = block if g == 0 else blocks + block
+            means = mean if g == 0 else means + mean
+        part_b[i, h] = (0.125 / GB) * blocks + (1.0 / GB) * means
         return _
 
     lax.fori_loop(0, n_i * upper, rounds_c_b, 0)
 
     def round_a(g, _):
+        peers = [(i, h) for i in range(n_i) for h in range(upper)]
+        slots = [slot(h * GB + g) for h in range(upper)]
+        means = [part_c[i, h * GB + g] for i, h in peers]
         for k in range(n_k):
             mixed = [
-                quarter[i, h * GB + g, k] + sum_b[i, h, k] for i in range(n_i) for h in range(upper)
+                0.125 * spread[i, slots[h], k] + (mean + part_b[i, h, k])
+                for (i, h), mean in zip(peers, means)
             ]
-            total = mixed[0]
-            for value in mixed[1:]:
-                total = total + value
-            total = total * (1.0 / group_a)
-            for i in range(n_i):
-                for h in range(upper):
-                    out[i, table[h * GB + g], k] = mixed[i * upper + h] + total
+            terms = mixed
+            while len(terms) > 1:
+                terms = [sum(terms[n : n + 2][1:], terms[n]) for n in range(0, len(terms), 2)]
+            total = terms[0] * (1.0 / len(peers))
+            for (i, h), value in zip(peers, mixed):
+                out[i, slots[h], k] = value + total
         return _
 
     lax.fori_loop(0, GB, round_a, 0)
 
 
 def on_device(grads, peer_table, layer_offsets):
-    n_i, n_p, n_k = (lax.axis_size(a) for a in AXES)
+    n_i, near, far, n_k = (lax.axis_size(a) for a in AXES)
+    n_p = near * far
     peers = n_i * n_p * n_k
     width = grads.shape[-1]
     columns = width // LANE
@@ -89,7 +100,7 @@
         in_specs=[SMEM, VMEM],
         out_specs=VMEM,
         scratch_shapes=[
-            pltpu.VMEM(block, jnp.float32),
+            pltpu.VMEM((n_i, n_p, per, LANE), jnp.float32),
             pltpu.VMEM((n_i, n_p // GB, n_k, per, LANE), jnp.float32),
         ],
         compiler_params=SMALL,
@@ -103,11 +114,9 @@
 
 
 def solution(mesh):
-    placed = (P("gx", "gy", "gz", None, None), P(), P())
+    gx, gy, gz = mesh.devices.shape
+    fine = Mesh(mesh.devices.reshape(gx, gy // NEAR, NEAR, gz), ("gx", "gy_far", "gy_near", "gz"))
+    spec = P("gx", ("gy_far", "gy_near"), "gz", None, None)
     return jax.shard_map(
-        on_device,
-        mesh=mesh,
-        in_specs=placed,
-        out_specs=P("gx", "gy", "gz", None, None),
-        check_vma=False,
+        on_device, mesh=fine, in_specs=(spec, P(), P()), out_specs=spec, check_vma=False
     )

time: 146 us -> 146 us (level)
  no operation moved by 1% of the time
where the time goes in v3:
time: 146 us
  blocking collectives  140 us (96%)
  Pallas kernels  3.9 us (3%)
    all_to_all x1, blocking collectives, on_device(): lax.all_to_all(tiles.reshape(peers, -1, LANE), AXES, split_axis=0, concat...  76.6 us
    all_to_all x1, blocking collectives, on_device(): lax.all_to_all(mixed.reshape(peers, per, LANE), AXES, split_axis=0, conca...  63.8 us

profile of v3, /device:TPU:1, one launch (start us, length us, event | category | flops | bytes accessed | tf_op | source)
XLA Modules:
  0.0 145.7 jit_solution(15489304828806702158)
XLA Ops:
  0.0 2.2 %pack.1 = f32[128,4096]{1,0:T(8,128)S(1)} custom-call(s32[2]{0:T(128)} %offsets.1, f32[1,1,1,160,4096]{4,3,2,1,0:T(8,128)} %grads.1), custom_call_target="tpu_custom_call" | custom-call | tf_op jit(solution)/shard_map/pack/pallas_call | solution.py:83
  2.2 0.0 copy-start
  2.2 76.6 %all_to_all.10 = f32[512,8,128]{2,1,0:T(8,128)S(1)} all-to-all(f32[512,8,128]{2,1,0:T(8,128)S(1)} %bitcast.12), channel_id=1, replica_groups=mesh['gx'=4,'gy_far'=2,'gy_near'=8,'gz'=8] {'gx','gy_near','gy_far','gz'}, dimensions={0} | all-to-all | bytes 4194304 | tf_op jit(solution)/shard_map/all_to_all | solution.py:92
  78.8 0.0 copy-done
  78.8 1.7 %mix.1 = f32[4,16,8,8,128]{4,3,2,1,0:T(8,128)S(1)} custom-call(s32[16]{0:T(128)S(1)} %copy-done, f32[4,16,8,8,128]{4,3,2,1,0:T(8,128)S(1)} %bitcast.13), custom_call_target="tpu_custom_call" | custom-call | tf_op jit(solution)/shard_map/mix/pallas_call | solution.py:97
  80.5 63.8 %all_to_all.11 = f32[512,8,128]{2,1,0:T(8,128)S(1)} all-to-all(f32[512,8,128]{2,1,0:T(8,128)S(1)} %bitcast.14), channel_id=1, replica_groups=mesh['gx'=4,'gy_far'=2,'gy_near'=8,'gz'=8] {'gx','gy_near','gy_far','gz'}, dimensions={0} | all-to-all | bytes 4194304 | tf_op jit(solution)/shard_map/all_to_all | solution.py:109
  144.3 1.3 copy.5
Async XLA Ops:
  2.2 76.6 %copy-start = (s32[16]{0:T(128)S(1)}, s32[16]{0:T(128)}, u32[]{:S(2)}) copy-start(s32[16]{0:T(128)} %table.1) | copy-start | bytes 196

commit v4 on v3

v4 whole, which is shorter than its diff:
```python
import jax
import jax.numpy as jnp
from jax import lax
from jax.experimental import pallas as pl
from jax.experimental.pallas import tpu as pltpu
from jax.sharding import Mesh
from jax.sharding import PartitionSpec as P

ROWS = 64
LAYERS = 2
GB = 8
SUB = 8
LANE = 128
NEAR = 8
AXES = ("gx", "gy_near", "gy_far", "gz")
VMEM = pl.BlockSpec(memory_space=pltpu.VMEM)
SMEM = pl.BlockSpec(memory_space=pltpu.SMEM)
ANY = pl.BlockSpec(memory_space=pl.ANY)
SMALL = pltpu.CompilerParams(vmem_limit_bytes=8 * 1024 * 1024)


def pack_kernel(offsets, grads, out, starts, rows, sems):
    part = rows.shape[0] // LAYERS
    copies = [pltpu.make_async_copy(offsets, starts, sems.at[LAYERS])]
    for layer in range(LAYERS):
        here = pl.ds(layer * part, part)
        copies.append(
            pltpu.make_async_copy(grads.at[0, 0, 0, here, :], rows.at[here, :], sems.at[layer])
        )
    for copy in copies:
        copy.start()
    copies[0].wait()
    for layer in range(LAYERS):
        start = pl.multiple_of(starts[layer], SUB)
        copies[layer + 1].wait()
        for line in range(0, ROWS, SUB):
            out[layer * ROWS + line : layer * ROWS + line + SUB, :] = rows[
                pl.ds(pl.multiple_of(start + line, SUB), SUB), :
            ]


def mix_kernel(table, spread, out, slots, part_c, part_b):
    n_i, n_p, n_k = spread.shape[:3]
    upper = n_p // GB
    far = n_p // NEAR
    for j in range(n_p):
        p = table[j]
        slots[j] = (p & (NEAR - 1)) * far + (p >> (NEAR.bit_length() - 1))

    def rounds_c_b(i, _):
        for h in range(upper):
            blocks, means = None, None
            for g in range(GB):
                block = spread[i, slots[h * GB + g]]
                mean = (0.125 / n_k) * jnp.sum(block, axis=0)
                part_c[i, h * GB + g] = mean
                blocks = block if g == 0 else blocks + block
                means = mean if g == 0 else means + mean
            part_b[i, h] = (0.125 / GB) * blocks + (1.0 / GB) * means
        return _

    lax.fori_loop(0, n_i, rounds_c_b, 0)

    def round_a(g, _):
        peers = [(i, h) for i in range(n_i) for h in range(upper)]
        mixed = [
            0.125 * spread[i, slots[h * GB + g]]
            + (part_b[i, h] + part_c[i, h * GB + g][None])
            for i, h in peers
        ]
        terms = mixed
        while len(terms) > 1:
            terms = [terms[n] + terms[n + 1] for n in range(0, len(terms), 2)]
        total = terms[0] * (1.0 / len(peers))
        for (i, h), value in zip(peers, mixed):
            out[i, slots[h * GB + g]] = value + total
        return _

    lax.fori_loop(0, GB, round_a, 0)


def on_device(grads, peer_table, layer_offsets):
    n_i, near, far, n_k = (lax.axis_size(a) for a in AXES)
    n_p = near * far
    peers = n_i * n_p * n_k
    width = grads.shape[-1]
    columns = width // LANE
    lines = ROWS * LAYERS
    packed = pl.pallas_call(
        pack_kernel,
        out_shape=pltpu.VMEM((lines, width), jnp.float32),
        in_specs=[ANY, ANY],
        out_specs=VMEM,
        scratch_shapes=[
            pltpu.SMEM(layer_offsets.shape, jnp.int32),
            pltpu.VMEM(grads.shape[-2:], jnp.float32),
            pltpu.SemaphoreType.DMA((LAYERS + 1,)),
        ],
        name="pack",
    )(layer_offsets, grads)
    tiles = packed.reshape(-1, SUB, columns, LANE).transpose(0, 2, 1, 3)
    spread = lax.all_to_all(
        tiles.reshape(peers, -1, LANE), AXES, split_axis=0, concat_axis=0, tiled=True
    )
    per = spread.shape[1]
    block = (n_i, n_p, n_k, per, LANE)
    mixed = pl.pallas_call(
        mix_kernel,
        out_shape=jax.ShapeDtypeStruct(block, jnp.float32),
        in_specs=[SMEM, VMEM],
        out_specs=VMEM,
        scratch_shapes=[
            pltpu.SMEM((n_p,), jnp.int32),
            pltpu.VMEM((n_i, n_p, per, LANE), jnp.float32),
            pltpu.VMEM((n_i, n_p // GB, n_k, per, LANE), jnp.float32),
        ],
        compiler_params=SMALL,
        name="mix",
    )(peer_table, spread.reshape(block))
    back = lax.all_to_all(
        mixed.reshape(peers, per, LANE), AXES, split_axis=0, concat_axis=0, tiled=True
    )
    tiles = back.reshape(-1, columns, SUB, LANE).transpose(0, 2, 1, 3)
    return tiles.reshape(1, 1, 1, lines, width)


def solution(mesh):
    gx, gy, gz = mesh.devices.shape
    fine = Mesh(mesh.devices.reshape(gx, gy // NEAR, NEAR, gz), ("gx", "gy_far", "gy_near", "gz"))
    spec = P("gx", ("gy_far", "gy_near"), "gz", None, None)
    return jax.shard_map(
        on_device, mesh=fine, in_specs=(spec, P(), P()), out_specs=spec, check_vma=False
    )
```

time: 146 us -> 145 us (level)
  no operation moved by 1% of the time
where the time goes in v4:
time: 145 us
  blocking collectives  140 us (97%)
  Pallas kernels  3.11 us (2%)
    all_to_all x1, blocking collectives, on_device(): lax.all_to_all(tiles.reshape(peers, -1, LANE), AXES, split_axis=0, concat...  76.6 us
    all_to_all x1, blocking collectives, on_device(): lax.all_to_all(mixed.reshape(peers, per, LANE), AXES, split_axis=0, conca...  63.8 us

profile of v4, /device:TPU:1, one launch (start us, length us, event | category | flops | bytes accessed | tf_op | source)
XLA Modules:
  0.0 144.9 jit_solution(14139235661656911838)
XLA Ops:
  0.0 1.8 %pack.1 = f32[128,4096]{1,0:T(8,128)S(1)} custom-call(s32[2]{0:T(128)} %offsets.1, f32[1,1,1,160,4096]{4,3,2,1,0:T(8,128)} %grads.1), custom_call_target="tpu_custom_call" | custom-call | tf_op jit(solution)/shard_map/pack/pallas_call | solution.py:89
  1.8 0.0 copy-start
  1.8 76.6 %all_to_all.10 = f32[512,8,128]{2,1,0:T(8,128)S(1)} all-to-all(f32[512,8,128]{2,1,0:T(8,128)S(1)} %bitcast.12), channel_id=1, replica_groups=mesh['gx'=4,'gy_far'=2,'gy_near'=8,'gz'=8] {'gx','gy_near','gy_far','gz'}, dimensions={0} | all-to-all | bytes 4194304 | tf_op jit(solution)/shard_map/all_to_all | solution.py:102
  78.4 0.0 copy-done
  78.4 1.3 mix.1
  79.7 63.8 %all_to_all.11 = f32[512,8,128]{2,1,0:T(8,128)S(1)} all-to-all(f32[512,8,128]{2,1,0:T(8,128)S(1)} %bitcast.14), channel_id=1, replica_groups=mesh['gx'=4,'gy_far'=2,'gy_near'=8,'gz'=8] {'gx','gy_near','gy_far','gz'}, dimensions={0} | all-to-all | bytes 4194304 | tf_op jit(solution)/shard_map/all_to_all | solution.py:120
  143.6 1.3 copy.5
Async XLA Ops:
  1.8 76.6 %copy-start = (s32[16]{0:T(128)S(1)}, s32[16]{0:T(128)}, u32[]{:S(2)}) copy-start(s32[16]{0:T(128)} %table.1) | copy-start | bytes 196

commit v5 on v4

--- a/solution.py
+++ b/solution.py
@@ -12,7 +12,8 @@
 SUB = 8
 LANE = 128
 NEAR = 8
-AXES = ("gx", "gy_near", "gy_far", "gz")
+CORES = 2
+AXES = ("gx", "gy_near", "gy_far", "gz_core", "gz_chip")
 VMEM = pl.BlockSpec(memory_space=pltpu.VMEM)
 SMEM = pl.BlockSpec(memory_space=pltpu.SMEM)
 ANY = pl.BlockSpec(memory_space=pl.ANY)
@@ -80,8 +81,8 @@
 
 
 def on_device(grads, peer_table, layer_offsets):
-    n_i, near, far, n_k = (lax.axis_size(a) for a in AXES)
-    n_p = near * far
+    n_i, near, far, cores, chips = (lax.axis_size(a) for a in AXES)
+    n_p, n_k = near * far, cores * chips
     peers = n_i * n_p * n_k
     width = grads.shape[-1]
     columns = width // LANE
@@ -126,8 +127,13 @@
 
 def solution(mesh):
     gx, gy, gz = mesh.devices.shape
-    fine = Mesh(mesh.devices.reshape(gx, gy // NEAR, NEAR, gz), ("gx", "gy_far", "gy_near", "gz"))
-    spec = P("gx", ("gy_far", "gy_near"), "gz", None, None)
+    names = ("gx", "gy_far", "gy_near", "gz_chip", "gz_core")
+    shape = (gx, gy // NEAR, NEAR, gz // CORES, CORES)
+    spec = P("gx", names[1:3], names[3:], None, None)
     return jax.shard_map(
-        on_device, mesh=fine, in_specs=(spec, P(), P()), out_specs=spec, check_vma=False
+        on_device,
+        mesh=Mesh(mesh.devices.reshape(shape), names),
+        in_specs=(spec, P(), P()),
+        out_specs=spec,
+        check_vma=False,
     )

time: 145 us -> 146 us (level)
  no operation moved by 1% of the time
where the time goes in v5:
time: 146 us
  blocking collectives  141 us (97%)
  Pallas kernels  3.11 us (2%)
    all_to_all x1, blocking collectives, on_device(): lax.all_to_all(tiles.reshape(peers, -1, LANE), AXES, split_axis=0, concat...  77.7 us
    all_to_all x1, blocking collectives, on_device(): lax.all_to_all(mixed.reshape(peers, per, LANE), AXES, split_axis=0, conca...  63.8 us

profile of v5, /device:TPU:1, one launch (start us, length us, event | category | flops | bytes accessed | tf_op | source)
XLA Modules:
  0.0 146.0 jit_solution(13148411426365063829)
XLA Ops:
  0.0 1.8 %pack.1 = f32[128,4096]{1,0:T(8,128)S(1)} custom-call(s32[2]{0:T(128)} %offsets.1, f32[1,1,1,160,4096]{4,3,2,1,0:T(8,128)} %grads.1), custom_call_target="tpu_custom_call" | custom-call | tf_op jit(solution)/shard_map/pack/pallas_call | solution.py:90
  1.8 0.0 copy-start
  1.8 77.7 %all_to_all.10 = f32[512,8,128]{2,1,0:T(8,128)S(1)} all-to-all(f32[512,8,128]{2,1,0:T(8,128)S(1)} %bitcast.12), channel_id=1, replica_groups=mesh['gx'=4,'gy_far'=2,'gy_near'=8,'gz_chip'=4,'gz_core'=2] {'gx','gy_ne..., dimensions={0} | all-to-all | bytes 4194304 | tf_op jit(solution)/shard_map/all_to_all | solution.py:103
  79.5 0.0 copy-done
  79.5 1.3 mix.1
  80.8 63.8 %all_to_all.11 = f32[512,8,128]{2,1,0:T(8,128)S(1)} all-to-all(f32[512,8,128]{2,1,0:T(8,128)S(1)} %bitcast.14), channel_id=1, replica_groups=mesh['gx'=4,'gy_far'=2,'gy_near'=8,'gz_chip'=4,'gz_core'=2] {'gx','gy_ne..., dimensions={0} | all-to-all | bytes 4194304 | tf_op jit(solution)/shard_map/all_to_all | solution.py:121
  144.6 1.3 copy.5
Async XLA Ops:
  1.8 77.7 %copy-start = (s32[16]{0:T(128)S(1)}, s32[16]{0:T(128)}, u32[]{:S(2)}) copy-start(s32[16]{0:T(128)} %table.1) | copy-start | bytes 196

commit v6 on v4

--- a/solution.py
+++ b/solution.py
@@ -3,7 +3,6 @@
 from jax import lax
 from jax.experimental import pallas as pl
 from jax.experimental.pallas import tpu as pltpu
-from jax.sharding import Mesh
 from jax.sharding import PartitionSpec as P
 
 ROWS = 64
@@ -11,8 +10,7 @@
 GB = 8
 SUB = 8
 LANE = 128
-NEAR = 8
-AXES = ("gx", "gy_near", "gy_far", "gz")
+AXES = ("gy", "gx", "gz")
 VMEM = pl.BlockSpec(memory_space=pltpu.VMEM)
 SMEM = pl.BlockSpec(memory_space=pltpu.SMEM)
 ANY = pl.BlockSpec(memory_space=pl.ANY)
@@ -39,19 +37,15 @@
             ]
 
 
-def mix_kernel(table, spread, out, slots, part_c, part_b):
-    n_i, n_p, n_k = spread.shape[:3]
+def mix_kernel(table, spread, out, part_c, part_b):
+    n_p, n_i, n_k = spread.shape[:3]
     upper = n_p // GB
-    far = n_p // NEAR
-    for j in range(n_p):
-        p = table[j]
-        slots[j] = (p & (NEAR - 1)) * far + (p >> (NEAR.bit_length() - 1))
 
     def rounds_c_b(i, _):
         for h in range(upper):
             blocks, means = None, None
             for g in range(GB):
-                block = spread[i, slots[h * GB + g]]
+                block = spread[table[h * GB + g], i]
                 mean = (0.125 / n_k) * jnp.sum(block, axis=0)
                 part_c[i, h * GB + g] = mean
                 blocks = block if g == 0 else blocks + block
@@ -64,7 +58,7 @@
     def round_a(g, _):
         peers = [(i, h) for i in range(n_i) for h in range(upper)]
         mixed = [
-            0.125 * spread[i, slots[h * GB + g]]
+            0.125 * spread[table[h * GB + g], i]
             + (part_b[i, h] + part_c[i, h * GB + g][None])
             for i, h in peers
         ]
@@ -73,15 +67,14 @@
             terms = [terms[n] + terms[n + 1] for n in range(0, len(terms), 2)]
         total = terms[0] * (1.0 / len(peers))
         for (i, h), value in zip(peers, mixed):
-            out[i, slots[h * GB + g]] = value + total
+            out[table[h * GB + g], i] = value + total
         return _
 
     lax.fori_loop(0, GB, round_a, 0)
 
 
 def on_device(grads, peer_table, layer_offsets):
-    n_i, near, far, n_k = (lax.axis_size(a) for a in AXES)
-    n_p = near * far
+    n_p, n_i, n_k = (lax.axis_size(a) for a in AXES)
     peers = n_i * n_p * n_k
     width = grads.shape[-1]
     columns = width // LANE
@@ -103,14 +96,13 @@
         tiles.reshape(peers, -1, LANE), AXES, split_axis=0, concat_axis=0, tiled=True
     )
     per = spread.shape[1]
-    block = (n_i, n_p, n_k, per, LANE)
+    block = (n_p, n_i, n_k, per, LANE)
     mixed = pl.pallas_call(
         mix_kernel,
         out_shape=jax.ShapeDtypeStruct(block, jnp.float32),
         in_specs=[SMEM, VMEM],
         out_specs=VMEM,
         scratch_shapes=[
-            pltpu.SMEM((n_p,), jnp.int32),
             pltpu.VMEM((n_i, n_p, per, LANE), jnp.float32),
             pltpu.VMEM((n_i, n_p // GB, n_k, per, LANE), jnp.float32),
         ],
@@ -125,9 +117,7 @@
 
 
 def solution(mesh):
-    gx, gy, gz = mesh.devices.shape
-    fine = Mesh(mesh.devices.reshape(gx, gy // NEAR, NEAR, gz), ("gx", "gy_far", "gy_near", "gz"))
-    spec = P("gx", ("gy_far", "gy_near"), "gz", None, None)
+    placed = P("gx", "gy", "gz", None, None)
     return jax.shard_map(
-        on_device, mesh=fine, in_specs=(spec, P(), P()), out_specs=spec, check_vma=False
+        on_device, mesh=mesh, in_specs=(placed, P(), P()), out_specs=placed, check_vma=False
     )

time: 145 us -> 145 us (level)
  no operation moved by 1% of the time
where the time goes in v6:
time: 145 us
  blocking collectives  140 us (97%)
  Pallas kernels  3.09 us (2%)
    all_to_all x1, blocking collectives, on_device(): lax.all_to_all(tiles.reshape(peers, -1, LANE), AXES, split_axis=0, concat...  75.9 us
    all_to_all x1, blocking collectives, on_device(): lax.all_to_all(mixed.reshape(peers, per, LANE), AXES, split_axis=0, conca...  64.3 us

profile of v6, /device:TPU:1, one launch (start us, length us, event | category | flops | bytes accessed | tf_op | source)
XLA Modules:
  0.0 144.7 jit_solution(8586372214864920514)
XLA Ops:
  0.0 1.8 %pack.1 = f32[128,4096]{1,0:T(8,128)S(1)} custom-call(s32[2]{0:T(128)} %offsets.1, f32[1,1,1,160,4096]{4,3,2,1,0:T(8,128)} %grads.1), custom_call_target="tpu_custom_call" | custom-call | tf_op jit(solution)/shard_map/pack/pallas_call | solution.py:82
  1.8 0.0 copy-start
  1.8 75.9 %all_to_all.10 = f32[512,8,128]{2,1,0:T(8,128)S(1)} all-to-all(f32[512,8,128]{2,1,0:T(8,128)S(1)} %bitcast.12), channel_id=1, replica_groups=mesh['gx'=4,'gy'=16,'gz'=8] {'gy','gx','gz'}, dimensions={0} | all-to-all | bytes 4194304 | tf_op jit(solution)/shard_map/all_to_all | solution.py:95
  77.7 0.0 copy-done
  77.7 1.3 mix.1
  79.0 64.3 %all_to_all.11 = f32[512,8,128]{2,1,0:T(8,128)S(1)} all-to-all(f32[512,8,128]{2,1,0:T(8,128)S(1)} %bitcast.14), channel_id=1, replica_groups=mesh['gx'=4,'gy'=16,'gz'=8] {'gy','gx','gz'}, dimensions={0} | all-to-all | bytes 4194304 | tf_op jit(solution)/shard_map/all_to_all | solution.py:112
  143.3 1.3 copy.5
Async XLA Ops:
  1.8 75.9 %copy-start = (s32[16]{0:T(128)S(1)}, s32[16]{0:T(128)}, u32[]{:S(2)}) copy-start(s32[16]{0:T(128)} %table.1) | copy-start | bytes 196
